TPU v7x, 32 devices: a whole 2x2x4 slice. The times are simulated.
32 devices in a mesh: col: 8 (over y, x, core), row: 4 (over z).
Axes of the slice: x: 2, y: 2, z: 4, core: 2. Of those that a mesh axis runs over, the one named last changes fastest.
Arguments:
- rhs: float32 [2, 32, 4, 4096], P(None, None, 'row', 'col'), may hold values from -6 to 6
- u_factor: bfloat16 [64, 40, 2, 256, 128], P('row', 'col'), may hold values from -0.078125 to 0.078125
- v_factor: bfloat16 [64, 40, 2, 256, 128], P('row', 'col'), may hold values from -0.375 to 0.375
- ranks: int32 [64, 40], P('row', 'col'), may hold values from 8 to 128, as said below
- assign: int32 [40], replicated, may hold values from 0 to 39, each once
Outputs:
- solution: float32 [2, 32, 10240], P(None, None, 'col')
- residual_estimate: float32 [32], replicated
Inputs may be any that keep to these rules, and one draw needn't show every extreme that they name: `ranks`: every entry is 128 // 16 times a power of two from 1 to 16.
All inputs are finite; a program needn't handle non-finite values.
Results may differ from a plain program's by a relative error of at most 0.0068.
Values may be sent and summed in bfloat16 or wider, within the bound.
No kernel may reach another device: no remote copies, remote signals or barrier semaphores. Data moves between devices by JAX's collectives and lax.ppermute only.
A program may use at most 128 MiB of HBM per device.

v0:
```python
import jax
import jax.numpy as jnp
from jax import lax
from jax.sharding import PartitionSpec as P

ITERS = 2


def sum_squares(value):
    return jnp.sum(value * value, axis=(0, 2))


def on_device(rhs, u_factor, v_factor, ranks, assign):
    tile_rows = u_factor.shape[0]
    tile_cols = u_factor.shape[1]
    tile_size = u_factor.shape[3]
    rank_cap = u_factor.shape[4]
    sources = rhs.shape[1]
    rank_iota = lax.broadcasted_iota(jnp.int32, (tile_rows, tile_cols, 1, 1, rank_cap), 4)
    mask = (rank_iota < ranks[:, :, None, None, None]).astype(jnp.float32)

    def adjoint_terms(group_data):
        data_b = group_data.reshape(2, sources, tile_rows, tile_size)
        raw = jnp.einsum("ipcnk,dsin->ipcdsk", u_factor, data_b, preferred_element_type=jnp.float32)
        coeff = jnp.stack(
            [raw[:, :, 0, 0] + raw[:, :, 1, 1], raw[:, :, 0, 1] - raw[:, :, 1, 0]], axis=2
        )
        coeff = (coeff * mask).astype(jnp.bfloat16)
        prod = jnp.einsum("ipcnk,ipdsk->cdspn", v_factor, coeff, preferred_element_type=jnp.float32)
        partial_model = jnp.stack([prod[0, 0] + prod[1, 1], prod[0, 1] - prod[1, 0]], axis=0)
        return partial_model.reshape(2, sources, tile_cols * tile_size)

    def adjoint_step(data_hat, v_prev):
        group_data = lax.all_gather(data_hat.astype(jnp.bfloat16), "col", axis=2, tiled=True)
        beta_now = jnp.sqrt(lax.psum(sum_squares(data_hat), ("col", "row")))
        model_sum = lax.psum(adjoint_terms(group_data), "row")
        v_hat = model_sum / beta_now[None, :, None] - beta_now[None, :, None] * v_prev
        alpha_now = jnp.sqrt(lax.psum(sum_squares(v_hat), "col"))
        return (
            data_hat / beta_now[None, :, None],
            beta_now,
            v_hat / alpha_now[None, :, None],
            alpha_now,
        )

    data_first = rhs.reshape(2, sources, rhs.shape[3])
    zero_model = jnp.zeros((2, sources, tile_cols * tile_size), jnp.float32)
    u_vec, beta_now, v_vec, alpha_now = adjoint_step(data_first, zero_model)
    w_vec = v_vec
    x_vec = zero_model
    phibar = beta_now
    rhobar = alpha_now
    for iteration in range(ITERS):
        model_b = v_vec.astype(jnp.bfloat16).reshape(2, sources, tile_cols, tile_size)
        forward_raw = jnp.einsum(
            "ipcnk,dspn->ipcdsk", v_factor, model_b, preferred_element_type=jnp.float32
        )
        forward_coeff = jnp.stack(
            [
                forward_raw[:, :, 0, 0] - forward_raw[:, :, 1, 1],
                forward_raw[:, :, 0, 1] + forward_raw[:, :, 1, 0],
            ],
            axis=2,
        )
        forward_coeff = (forward_coeff * mask).astype(jnp.bfloat16)
        forward_prod = jnp.einsum(
            "ipcnk,ipdsk->cdsin", u_factor, forward_coeff, preferred_element_type=jnp.float32
        )
        partial_data = jnp.stack(
            [forward_prod[0, 0] - forward_prod[1, 1], forward_prod[0, 1] + forward_prod[1, 0]],
            axis=0,
        )
        partial_data = partial_data.reshape(2, sources, tile_rows * tile_size)
        data_hat = (
            lax.psum_scatter(partial_data, "col", scatter_dimension=2, tiled=True)
            - alpha_now[None, :, None] * u_vec
        )
        u_vec, beta_now, v_vec, alpha_now = adjoint_step(data_hat, v_vec)
        rho_now = jnp.sqrt(rhobar * rhobar + beta_now * beta_now)
        cosine = rhobar / rho_now
        sine = beta_now / rho_now
        theta = sine * alpha_now
        rhobar = -cosine * alpha_now
        phi_now = cosine * phibar
        phibar = sine * phibar
        x_vec = x_vec + (phi_now / rho_now)[None, :, None] * w_vec
        w_vec = v_vec - (theta / rho_now)[None, :, None] * w_vec
    all_cols = assign.shape[0]
    natural = lax.axis_index("col") * tile_cols + jnp.arange(tile_cols, dtype=jnp.int32)
    positions = jnp.arange(all_cols, dtype=jnp.int32)
    where_held = jnp.sum(
        positions[None, :] * (assign[None, :] == natural[:, None]).astype(jnp.int32), axis=1
    )
    share = sources // lax.axis_size("row")
    own_share = lax.dynamic_slice_in_dim(x_vec, lax.axis_index("row") * share, share, 1)
    gathered = lax.all_gather(own_share, "col", axis=2, tiled=True)
    gathered = gathered.reshape(2, share, all_cols, tile_size)
    picked = jnp.take(gathered, where_held, axis=2).reshape(2, share, tile_cols * tile_size)
    solution = lax.all_gather(picked, "row", axis=1, tiled=True)
    return (solution, phibar)


def solution(mesh):
    in_specs = (
        P(None, None, "row", "col"),
        P("row", "col", None, None, None),
        P("row", "col", None, None, None),
        P("row", "col"),
        P(),
    )
    out_specs = (P(None, None, "col"), P())
    return jax.shard_map(
        on_device, mesh=mesh, in_specs=in_specs, out_specs=out_specs, check_vma=False
    )
```

profile of v0, /device:TPU:0, one launch (start us, length us, event | category | flops | bytes accessed | tf_op | source)
XLA Modules:
  0.0 338.9 jit_solution(15961958501180942365)
XLA Ops:
  7.2 0.9 copy.217
  8.1 11.3 %all_gather.12 = bf16[2,32,4096]{2,1,0:T(8,128)(2,1)S(1)} all-gather(bf16[2,32,512]{2,1,0:T(8,128)(2,1)S(1)} %bitcast.164), channel_id=1, replica_groups=mesh['col'=8,'row'=4] {'col'}, dimensions={2}, use_global_device_ids=true | all-gather | bytes 589824 | tf_op jit(solution)/shard_map/all_gather | solution.py:34
  19.6 6.1 %fusion.29 = f32[16,5,2,2,32,128]{5,4,2,1,3,0:T(8,128)S(1)} fusion(bf16[16,5,2,256,128]{4,3,2,1,0:T(8,128)(2,1)} %param.6, bf16[2,32,16,256,1,1]{3,2,1,0,5,4:T(8,128)(2,1)S(1)} %bitcast_bitcast_fusion.1), kind=kOutput, calls=%fused_computation.28 | convolution fusion | flops 671088640 | bytes 16252928 | tf_op jit(solution)/shard_map/ipcnk,dsin->ipcdsk/dot_general | solution.py:24
  26.8 5.9 %fusion.55 = f32[2,2,32,5,256]{4,2,0,1,3:T(8,128)S(1)} fusion(bf16[16,5,2,256,128]{4,3,2,1,0:T(8,128)(2,1)} %param.7, f32[16,5,1,32,128]{4,3,1,0,2:T(8,128)S(1)} %fusion.48, f32[16,5,1,32,128]{4,3,1,0,2:T(8,128)S(1)} %fusion.50, f32[16,5,128]{2,1,0:T(8,128)S(1)} %fusion.74), kind=kOutput, calls=%fused_computation.57 | convolution fusion | flops 673054720 | bytes 13803520 | tf_op jit(solution)/shard_map/ipcnk,ipdsk->cdspn/dot_general | solution.py:29
  33.2 0.7 pad_maximum_fusion.2
  34.1 39.7 %psum.50 = f32[32]{0:T(128)S(1)} all-reduce(f32[32]{0:T(128)S(1)} %fusion.69), channel_id=1, replica_groups=mesh['col'=8,'row'=4] {'col','row'}, use_global_device_ids=true, to_apply=%region_3.0 | all-reduce | flops 32 | bytes 256 | tf_op jit(solution)/shard_map/psum | solution.py:35
  73.9 1.2 multiply_reduce_fusion.1
  75.1 12.7 %psum.51 = f32[32]{0:T(128)S(1)} all-reduce(f32[32]{0:T(128)S(1)} %multiply_reduce_fusion.1), channel_id=1, replica_groups=mesh['col'=8,'row'=4] {'col'}, use_global_device_ids=true, to_apply=%region_5.0 | all-reduce | flops 32 | bytes 256 | tf_op jit(solution)/shard_map/psum | solution.py:38
  87.8 1.2 fusion.78
  89.2 5.2 %fusion.20 = f32[16,5,2,2,32,128]{5,4,1,0,3,2:T(8,128)S(1)} fusion(bf16[2,32,5,256,1,1]{3,2,1,0,5,4:T(8,128)(2,1)S(1)} %bitcast.160, bf16[16,5,2,256,128]{4,3,2,1,0:T(8,128)(2,1)} %param.7), kind=kOutput, calls=%fused_computation.25 | convolution fusion | flops 671088640 | bytes 15892480 | tf_op jit(solution)/shard_map/ipcnk,dspn->ipcdsk/dot_general | solution.py:55
  94.5 1.7 fusion.47
  96.2 4.6 %fusion.32 = f32[2,2,32,16,256]{4,2,0,1,3:T(8,128)S(1)} fusion(bf16[16,5,2,256,128]{4,3,2,1,0:T(8,128)(2,1)S(1)} %bitcast.150, f32[16,5,1,32,128]{4,3,1,0,2:T(8,128)} %get-tuple-element.17, f32[16,5,1,32,128]{4,3,1,0,2:T(8,128)S(1)} %get-tuple-element.16, f32[16,5,128]{2,1,0:T(8,128)S(1)} %fusion.74), kind=kOutput, calls=%fused_computation.29 | convolution fusion | flops 673054720 | bytes 15245312 | tf_op jit(solution)/shard_map/ipcnk,ipdsk->cdsin/dot_general | solution.py:66
  101.8 1.0 pad_maximum_fusion
  102.9 35.1 %reduce-scatter.3.cloned.1.call-done = f32[2,32,512]{2,1,0:T(8,128)} async-done(((f32[2,32,4096]{2,1,0:T(8,128)}), f32[2,32,512]{2,1,0:T(8,128)}) %reduce-scatter.3.cloned.1.call-update) | async-done | bytes 131088 | tf_op jit(solution)/shard_map/reduce_scatter | solution.py:75
  138.0 1.1 multiply_reduce_fusion.3
  139.1 10.0 %all_gather.13 = bf16[2,32,4096]{2,1,0:T(8,128)(2,1)S(1)} all-gather(bf16[2,32,512]{2,1,0:T(8,128)(2,1)S(1)} %convert_element_type.38), channel_id=1, replica_groups=mesh['col'=8,'row'=4] {'col'}, dimensions={2}, use_global_device_ids=true | all-gather | bytes 589824 | tf_op jit(solution)/shard_map/all_gather | solution.py:34
  149.3 5.2 %fusion.26 = f32[16,5,2,2,32,128]{5,4,1,0,3,2:T(8,128)S(1)} fusion(bf16[2,32,16,256,1,1]{3,2,1,0,5,4:T(8,128)(2,1)S(1)} %bitcast_bitcast_fusion, bf16[16,5,2,256,128]{4,3,2,1,0:T(8,128)(2,1)} %param.6), kind=kOutput, calls=%fused_computation.27 | convolution fusion | flops 671088640 | bytes 16252928 | tf_op jit(solution)/shard_map/ipcnk,dsin->ipcdsk/dot_general | solution.py:24
  156.3 3.3 fusion.60
  159.9 0.7 pad_maximum_fusion.3
  160.8 39.6 %psum.52 = f32[32]{0:T(128)S(1)} all-reduce(f32[32]{0:T(128)S(1)} %get-tuple-element.8), channel_id=1, replica_groups=mesh['col'=8,'row'=4] {'col','row'}, use_global_device_ids=true, to_apply=%region_8.0 | all-reduce | flops 32 | bytes 256 | tf_op jit(solution)/shard_map/psum | solution.py:35
  200.4 1.4 multiply_reduce_fusion
  201.7 12.7 %psum.54 = f32[32]{0:T(128)S(1)} all-reduce(f32[32]{0:T(128)S(1)} %multiply_reduce_fusion), channel_id=1, replica_groups=mesh['col'=8,'row'=4] {'col'}, use_global_device_ids=true, to_apply=%region_11.0 | all-reduce | flops 32 | bytes 256 | tf_op jit(solution)/shard_map/psum | solution.py:38
  214.4 1.1 fusion.76
  215.8 5.2 %fusion.23 = f32[16,5,2,2,32,128]{5,4,1,0,3,2:T(8,128)S(1)} fusion(bf16[2,32,5,256,1,1]{3,2,1,0,5,4:T(8,128)(2,1)S(1)} %bitcast.161, bf16[16,5,2,256,128]{4,3,2,1,0:T(8,128)(2,1)} %param.7), kind=kOutput, calls=%fused_computation.26 | convolution fusion | flops 671088640 | bytes 15892480 | tf_op jit(solution)/shard_map/ipcnk,dspn->ipcdsk/dot_general | solution.py:55
  221.0 1.7 fusion.43
  222.7 4.6 %fusion.35 = f32[2,2,32,16,256]{4,2,0,1,3:T(8,128)S(1)} fusion(bf16[16,5,2,256,128]{4,3,2,1,0:T(8,128)(2,1)S(1)} %bitcast.152, f32[16,5,1,32,128]{4,3,1,0,2:T(8,128)} %get-tuple-element.13, f32[16,5,1,32,128]{4,3,1,0,2:T(8,128)S(1)} %get-tuple-element.12, f32[16,5,128]{2,1,0:T(8,128)S(1)} %fusion.74), kind=kOutput, calls=%fused_computation.30 | convolution fusion | flops 673054720 | bytes 15245312 | tf_op jit(solution)/shard_map/ipcnk,ipdsk->cdsin/dot_general | solution.py:66
  228.3 1.0 pad_maximum_fusion.1
  229.7 34.9 %reduce-scatter.5.cloned.1.call-done = f32[2,32,512]{2,1,0:T(8,128)} async-done(((f32[2,32,4096]{2,1,0:T(8,128)}), f32[2,32,512]{2,1,0:T(8,128)}) %reduce-scatter.5.cloned.1.call-update) | async-done | bytes 131088 | tf_op jit(solution)/shard_map/reduce_scatter | solution.py:75
  264.6 1.1 multiply_reduce_fusion.2
  265.7 39.3 %psum.55 = f32[32]{0:T(128)S(1)} all-reduce(f32[32]{0:T(128)S(1)} %multiply_reduce_fusion.2), channel_id=1, replica_groups=mesh['col'=8,'row'=4] {'col','row'}, use_global_device_ids=true, to_apply=%region_14.0 | all-reduce | flops 32 | bytes 256 | tf_op jit(solution)/shard_map/psum | solution.py:35
  305.9 10.9 %all_gather.14 = f32[2,8,10240]{2,1,0:T(8,128)S(1)} all-gather(f32[2,8,1280]{2,1,0:T(8,128)S(1)} %fusion.73), channel_id=1, replica_groups=mesh['col'=8,'row'=4] {'col'}, dimensions={2}, use_global_device_ids=true | all-gather | bytes 737280 | tf_op jit(solution)/shard_map/all_gather | solution.py:96
  317.4 14.3 %all_gather.15 = f32[2,32,1280]{2,1,0:T(8,128)S(1)} all-gather(f32[2,8,1280]{2,1,0:T(8,128)S(1)} %broadcast_select_fusion), channel_id=1, replica_groups=mesh['col'=8,'row'=4] {'row'}, dimensions={1}, use_global_device_ids=true | all-gather | bytes 409600 | tf_op jit(solution)/shard_map/all_gather | solution.py:99
  (91 shorter events, 9.2 us)
Async XLA Ops:
  7.2 66.7 %all-reduce.3.cloned.1.call-start = ((), (), s32[]{:S(2)}) async-start(), calls=%async_computation.2 | async-start | bytes 655360 | tf_op jit(solution)/shard_map/psum | solution.py:36
  26.0 0.7 copy-start.1
  32.7 1.3 copy-start
  33.9 104.1 %reduce-scatter.3.cloned.1.call-start = ((), (), s32[]{:S(2)}) async-start(), calls=%async_computation.3 | async-start | bytes 1179648 | tf_op jit(solution)/shard_map/reduce_scatter | solution.py:75
  87.8 8.4 %slice-start = ((s8[10485760]{0:T(1024)(128)(4,1)}), s8[2097152]{0:T(1024)(128)(4,1)S(1)}, s32[]{:S(2)}) async-start(s8[10485760]{0:T(1024)(128)(4,1)} %bitcast.149), calls=%async_computation.6 | async-start | bytes 4194304
  89.2 6.9 %slice-start.1 = ((s8[10485760]{0:T(1024)(128)(4,1)}), s8[4194304]{0:T(1024)(128)(4,1)S(1)}, s32[]{:S(2)}) async-start(s8[10485760]{0:T(1024)(128)(4,1)} %bitcast.149), calls=%async_computation.7 | async-start | bytes 8388608
  89.2 6.9 %slice-start.2 = ((s8[10485760]{0:T(1024)(128)(4,1)}), s8[4194304]{0:T(1024)(128)(4,1)S(1)}, s32[]{:S(2)}) async-start(s8[10485760]{0:T(1024)(128)(4,1)} %bitcast.149), calls=%async_computation.8 | async-start | bytes 8388608
  102.8 97.5 %all-reduce.5.cloned.1.call-start = ((), (), s32[]{:S(2)}) async-start(), calls=%async_computation.4 | async-start | bytes 655360 | tf_op jit(solution)/shard_map/psum | solution.py:36
  149.1 6.0 %slice-start.6 = ((s8[10485760]{0:T(1024)(128)(4,1)}), s8[4194304]{0:T(1024)(128)(4,1)S(1)}, s32[]{:S(2)}) async-start(s8[10485760]{0:T(1024)(128)(4,1)} %bitcast.153), calls=%async_computation.12 | async-start | bytes 8388608
  149.3 6.4 %slice-start.7 = ((s8[10485760]{0:T(1024)(128)(4,1)}), s8[4194304]{0:T(1024)(128)(4,1)S(1)}, s32[]{:S(2)}) async-start(s8[10485760]{0:T(1024)(128)(4,1)} %bitcast.153), calls=%async_computation.13 | async-start | bytes 8388608
  149.3 7.0 %slice-start.8 = ((s8[10485760]{0:T(1024)(128)(4,1)}), s8[2097152]{0:T(1024)(128)(4,1)S(1)}, s32[]{:S(2)}) async-start(s8[10485760]{0:T(1024)(128)(4,1)} %bitcast.153), calls=%async_computation.14 | async-start | bytes 4194304
  160.7 103.9 %reduce-scatter.5.cloned.1.call-start = ((), (), s32[]{:S(2)}) async-start(), calls=%async_computation.5 | async-start | bytes 1179648 | tf_op jit(solution)/shard_map/reduce_scatter | solution.py:75
  200.4 22.3 %slice-start.3 = ((s8[10485760]{0:T(1024)(128)(4,1)}), s8[2097152]{0:T(1024)(128)(4,1)S(1)}, s32[]{:S(2)}) async-start(s8[10485760]{0:T(1024)(128)(4,1)} %bitcast.151), calls=%async_computation.9 | async-start | bytes 4194304
  215.7 6.9 %slice-start.4 = ((s8[10485760]{0:T(1024)(128)(4,1)}), s8[4194304]{0:T(1024)(128)(4,1)S(1)}, s32[]{:S(2)}) async-start(s8[10485760]{0:T(1024)(128)(4,1)} %bitcast.151), calls=%async_computation.10 | async-start | bytes 8388608
  215.7 6.9 %slice-start.5 = ((s8[10485760]{0:T(1024)(128)(4,1)}), s8[4194304]{0:T(1024)(128)(4,1)S(1)}, s32[]{:S(2)}) async-start(s8[10485760]{0:T(1024)(128)(4,1)} %bitcast.151), calls=%async_computation.11 | async-start | bytes 8388608
  227.9 1.5 copy-start.2
Sparse Core Ops, SparseCore 0:
  34.0 36.6 all-reduce.2
  103.0 34.9 reduce-scatter.2
  160.8 36.2 all-reduce.4
  229.5 35.0 reduce-scatter.4
where the time goes:
time: 340 us; the launch traced here: 339 us
  blocking collectives  190 us (56%)
  waiting for transfers between devices  70.1 us (21%)
  matrix products  40 us (12%)
  other arithmetic  16.8 us (5%)
  between operations  14.3 us (4%)
  local copies, waits for them, and re-layouts  7.14 us (2%)
    psum x3, blocking collectives, adjoint_step(): beta_now = jnp.sqrt(lax.psum(sum_squares(data_hat), ('col', 'row')))  119 us
    reduce_scatter x2, waiting for transfers between devices, on_device(): lax.psum_scatter(partial_data, 'col', scatter_dimension=2, tiled=True)  70 us
    psum x2, blocking collectives, adjoint_step(): alpha_now = jnp.sqrt(lax.psum(sum_squares(v_hat), 'col'))  25.4 us
    all_gather x2, blocking collectives, adjoint_step(): lax.all_gather(data_hat.astype(jnp.bfloat16), 'col', axis=2, tiled=True)  21.3 us
    all_gather x1, blocking collectives, on_device(): solution = lax.all_gather(picked, 'row', axis=1, tiled=True)  14.3 us
    dot_general x2, matrix products, adjoint_terms(): jnp.einsum('ipcnk,dsin->ipcdsk', u_factor, data_b, preferred_element_type...  11.3 us
    all_gather x1, blocking collectives, on_device(): gathered = lax.all_gather(own_share, 'col', axis=2, tiled=True)  10.9 us
    dot_general x2, matrix products, on_device(): jnp.einsum('ipcnk,dspn->ipcdsk', v_factor, model_b, preferred_element_typ...  10.4 us
  transfers between devices with their start and end apart: 4, of which 2 were waited for; matrix products, arithmetic and copies ran while one was open for 0% of the time, Pallas kernels for 0%

commit v1 on v0

--- a/solution.py
+++ b/solution.py
@@ -1,9 +1,18 @@
+import functools
 import jax
 import jax.numpy as jnp
 from jax import lax
 from jax.sharding import PartitionSpec as P
 
 ITERS = 2
+
+
+def compute_zone(z, mesh_ax, axis_id):
+    local_part = lax.psum(lax.psum(z, mesh_ax), axis_id)
+    return local_part
+
+
+get_classes = functools.partial(compute_zone, mesh_ax="row", axis_id="col")
 
 
 def sum_squares(value):
@@ -32,7 +41,7 @@
 
     def adjoint_step(data_hat, v_prev):
         group_data = lax.all_gather(data_hat.astype(jnp.bfloat16), "col", axis=2, tiled=True)
-        beta_now = jnp.sqrt(lax.psum(sum_squares(data_hat), ("col", "row")))
+        beta_now = jnp.sqrt(get_classes(sum_squares(data_hat)))
         model_sum = lax.psum(adjoint_terms(group_data), "row")
         v_hat = model_sum / beta_now[None, :, None] - beta_now[None, :, None] * v_prev
         alpha_now = jnp.sqrt(lax.psum(sum_squares(v_hat), "col"))

time: 340 us -> 315 us (0.926)
  blocking collectives: 190 us -> 141 us
  waiting for transfers between devices: 70.1 us -> 95.3 us
    psum x3 -> x6, blocking collectives: 119 us -> 70.9 us  [compute_zone(): local_part = lax.psum(lax.psum(z, mesh_ax), axis_id)]
    psum x2, waiting for transfers between devices: 0.01 us -> 25.6 us  [adjoint_step(): model_sum = lax.psum(adjoint_terms(group_data), 'row')]
  transfers between devices with their start and end apart: 4 -> 4, of which waited for: 2 -> 4; matrix products, arithmetic and copies ran while one was open for 0% -> 0% of each run, Pallas kernels for 0% -> 0%
where the time goes in v1:
time: 315 us; the launch traced here: 314 us
  blocking collectives  141 us (45%)
  waiting for transfers between devices  95.3 us (30%)
  matrix products  40 us (13%)
  other arithmetic  16.9 us (5%)
  between operations  14.2 us (5%)
  local copies, waits for them, and re-layouts  7.14 us (2%)
    psum x6, blocking collectives, compute_zone(): local_part = lax.psum(lax.psum(z, mesh_ax), axis_id)  70.9 us
    reduce_scatter x2, waiting for transfers between devices, on_device(): lax.psum_scatter(partial_data, 'col', scatter_dimension=2, tiled=True)  69.6 us
    psum x2, waiting for transfers between devices, adjoint_step(): model_sum = lax.psum(adjoint_terms(group_data), 'row')  25.6 us
    psum x2, blocking collectives, adjoint_step(): alpha_now = jnp.sqrt(lax.psum(sum_squares(v_hat), 'col'))  23.7 us
    all_gather x2, blocking collectives, adjoint_step(): lax.all_gather(data_hat.astype(jnp.bfloat16), 'col', axis=2, tiled=True)  21.3 us
    all_gather x1, blocking collectives, on_device(): solution = lax.all_gather(picked, 'row', axis=1, tiled=True)  14.8 us
    dot_general x2, matrix products, adjoint_terms(): jnp.einsum('ipcnk,dsin->ipcdsk', u_factor, data_b, preferred_element_type...  11.3 us
    dot_general x2, matrix products, on_device(): jnp.einsum('ipcnk,dspn->ipcdsk', v_factor, model_b, preferred_element_typ...  10.4 us
  transfers between devices with their start and end apart: 4, of which 4 were waited for; matrix products, arithmetic and copies ran while one was open for 0% of the time, Pallas kernels for 0%

profile of v1, /device:TPU:0, one launch (start us, length us, event | category | flops | bytes accessed | tf_op | source)
XLA Modules:
  0.0 314.5 jit_solution(141301255224520776)
XLA Ops:
  8.1 11.3 %all_gather.12 = bf16[2,32,4096]{2,1,0:T(8,128)(2,1)S(1)} all-gather(bf16[2,32,512]{2,1,0:T(8,128)(2,1)S(1)} %bitcast.164), channel_id=1, replica_groups=mesh['col'=8,'row'=4] {'col'}, dimensions={2}, use_global_device_ids=true | all-gather | bytes 589824 | tf_op jit(solution)/shard_map/all_gather | solution.py:43
  19.6 6.1 %fusion.29 = f32[16,5,2,2,32,128]{5,4,2,1,3,0:T(8,128)S(1)} fusion(bf16[16,5,2,256,128]{4,3,2,1,0:T(8,128)(2,1)} %param.6, bf16[2,32,16,256,1,1]{3,2,1,0,5,4:T(8,128)(2,1)S(1)} %bitcast_bitcast_fusion.1), kind=kOutput, calls=%fused_computation.28 | convolution fusion | flops 671088640 | bytes 16252928 | tf_op jit(solution)/shard_map/ipcnk,dsin->ipcdsk/dot_general | solution.py:33
  26.8 5.9 %fusion.55 = f32[2,2,32,5,256]{4,2,0,1,3:T(8,128)S(1)} fusion(bf16[16,5,2,256,128]{4,3,2,1,0:T(8,128)(2,1)} %param.7, f32[16,5,1,32,128]{4,3,1,0,2:T(8,128)S(1)} %fusion.48, f32[16,5,1,32,128]{4,3,1,0,2:T(8,128)S(1)} %fusion.50, f32[16,5,128]{2,1,0:T(8,128)S(1)} %fusion.74), kind=kOutput, calls=%fused_computation.57 | convolution fusion | flops 673054720 | bytes 13803520 | tf_op jit(solution)/shard_map/ipcnk,ipdsk->cdspn/dot_general | solution.py:38
  34.1 12.1 %psum.71 = f32[32]{0:T(128)S(1)} all-reduce(f32[32]{0:T(128)S(1)} %fusion.69), channel_id=1, replica_groups=mesh['col'=8,'row'=4] {'row'}, use_global_device_ids=true, to_apply=%region_3.0 | all-reduce | flops 32 | bytes 256 | tf_op jit(solution)/shard_map/psum | solution.py:11
  46.2 11.8 %psum.72 = f32[32]{0:T(128)S(1)} all-reduce(f32[32]{0:T(128)S(1)} %psum.71), channel_id=1, replica_groups=mesh['col'=8,'row'=4] {'col'}, use_global_device_ids=true, to_apply=%region_4.0 | all-reduce | flops 32 | bytes 256 | tf_op jit(solution)/shard_map/psum | solution.py:11
  58.0 12.7 %all-reduce.3.cloned.1.call-done = f32[2,32,1280]{2,1,0:T(8,128)} async-done(((f32[2,32,1280]{2,1,0:T(8,128)}), f32[2,32,1280]{2,1,0:T(8,128)}) %all-reduce.3.cloned.1.call-update) | async-done | bytes 327696 | tf_op jit(solution)/shard_map/psum | solution.py:45
  70.7 1.2 multiply_reduce_fusion.1
  71.9 11.8 %psum.73 = f32[32]{0:T(128)S(1)} all-reduce(f32[32]{0:T(128)S(1)} %multiply_reduce_fusion.1), channel_id=1, replica_groups=mesh['col'=8,'row'=4] {'col'}, use_global_device_ids=true, to_apply=%region_6.0 | all-reduce | flops 32 | bytes 256 | tf_op jit(solution)/shard_map/psum | solution.py:47
  83.7 1.2 fusion.78
  85.2 5.2 %fusion.20 = f32[16,5,2,2,32,128]{5,4,1,0,3,2:T(8,128)S(1)} fusion(bf16[2,32,5,256,1,1]{3,2,1,0,5,4:T(8,128)(2,1)S(1)} %bitcast.160, bf16[16,5,2,256,128]{4,3,2,1,0:T(8,128)(2,1)} %param.7), kind=kOutput, calls=%fused_computation.25 | convolution fusion | flops 671088640 | bytes 15892480 | tf_op jit(solution)/shard_map/ipcnk,dspn->ipcdsk/dot_general | solution.py:64
  90.4 1.7 fusion.47
  92.1 4.6 %fusion.32 = f32[2,2,32,16,256]{4,2,0,1,3:T(8,128)S(1)} fusion(bf16[16,5,2,256,128]{4,3,2,1,0:T(8,128)(2,1)S(1)} %bitcast.150, f32[16,5,1,32,128]{4,3,1,0,2:T(8,128)} %get-tuple-element.17, f32[16,5,1,32,128]{4,3,1,0,2:T(8,128)S(1)} %get-tuple-element.16, f32[16,5,128]{2,1,0:T(8,128)S(1)} %fusion.74), kind=kOutput, calls=%fused_computation.29 | convolution fusion | flops 673054720 | bytes 15245312 | tf_op jit(solution)/shard_map/ipcnk,ipdsk->cdsin/dot_general | solution.py:75
  98.8 34.9 %reduce-scatter.3.cloned.1.call-done = f32[2,32,512]{2,1,0:T(8,128)} async-done(((f32[2,32,4096]{2,1,0:T(8,128)}), f32[2,32,512]{2,1,0:T(8,128)}) %reduce-scatter.3.cloned.1.call-update) | async-done | bytes 131088 | tf_op jit(solution)/shard_map/reduce_scatter | solution.py:84
  133.8 1.1 multiply_reduce_fusion.3
  134.9 10.0 %all_gather.13 = bf16[2,32,4096]{2,1,0:T(8,128)(2,1)S(1)} all-gather(bf16[2,32,512]{2,1,0:T(8,128)(2,1)S(1)} %convert_element_type.38), channel_id=1, replica_groups=mesh['col'=8,'row'=4] {'col'}, dimensions={2}, use_global_device_ids=true | all-gather | bytes 589824 | tf_op jit(solution)/shard_map/all_gather | solution.py:43
  145.1 5.2 %fusion.26 = f32[16,5,2,2,32,128]{5,4,1,0,3,2:T(8,128)S(1)} fusion(bf16[2,32,16,256,1,1]{3,2,1,0,5,4:T(8,128)(2,1)S(1)} %bitcast_bitcast_fusion, bf16[16,5,2,256,128]{4,3,2,1,0:T(8,128)(2,1)} %param.6), kind=kOutput, calls=%fused_computation.27 | convolution fusion | flops 671088640 | bytes 16252928 | tf_op jit(solution)/shard_map/ipcnk,dsin->ipcdsk/dot_general | solution.py:33
  152.1 3.3 %fusion.60 = f32[2,2,32,5,256]{4,2,0,1,3:T(8,128)S(1)} fusion(bf16[16,5,2,256,128]{4,3,2,1,0:T(8,128)(2,1)S(1)} %bitcast.154, f32[16,5,1,32,128]{4,3,1,0,2:T(8,128)S(1)} %get-tuple-element.15, f32[16,5,1,32,128]{4,3,1,0,2:T(8,128)S(1)} %get-tuple-element.14, f32[16,5,128]{2,1,0:T(8,128)S(1)} %fusion.74), kind=kOutput, calls=%fused_computation.58 | convolution fusion | flops 673054720 | bytes 13803520 | tf_op jit(solution)/shard_map/ipcnk,ipdsk->cdspn/dot_general | solution.py:38
  156.6 11.8 %psum.74 = f32[32]{0:T(128)S(1)} all-reduce(f32[32]{0:T(128)S(1)} %get-tuple-element.8), channel_id=1, replica_groups=mesh['col'=8,'row'=4] {'row'}, use_global_device_ids=true, to_apply=%region_9.0 | all-reduce | flops 32 | bytes 256 | tf_op jit(solution)/shard_map/psum | solution.py:11
  168.4 11.8 %psum.75 = f32[32]{0:T(128)S(1)} all-reduce(f32[32]{0:T(128)S(1)} %psum.74), channel_id=1, replica_groups=mesh['col'=8,'row'=4] {'col'}, use_global_device_ids=true, to_apply=%region_10.0 | all-reduce | flops 32 | bytes 256 | tf_op jit(solution)/shard_map/psum | solution.py:11
  180.2 12.9 %all-reduce.5.cloned.1.call-done = f32[2,32,1280]{2,1,0:T(8,128)} async-done(((f32[2,32,1280]{2,1,0:T(8,128)}), f32[2,32,1280]{2,1,0:T(8,128)}) %all-reduce.5.cloned.1.call-update) | async-done | bytes 327696 | tf_op jit(solution)/shard_map/psum | solution.py:45
  193.1 1.4 multiply_reduce_fusion
  194.4 11.8 %psum.77 = f32[32]{0:T(128)S(1)} all-reduce(f32[32]{0:T(128)S(1)} %multiply_reduce_fusion), channel_id=1, replica_groups=mesh['col'=8,'row'=4] {'col'}, use_global_device_ids=true, to_apply=%region_13.0 | all-reduce | flops 32 | bytes 256 | tf_op jit(solution)/shard_map/psum | solution.py:47
  206.3 1.1 fusion.76
  207.6 5.2 %fusion.23 = f32[16,5,2,2,32,128]{5,4,1,0,3,2:T(8,128)S(1)} fusion(bf16[2,32,5,256,1,1]{3,2,1,0,5,4:T(8,128)(2,1)S(1)} %bitcast.161, bf16[16,5,2,256,128]{4,3,2,1,0:T(8,128)(2,1)} %param.7), kind=kOutput, calls=%fused_computation.26 | convolution fusion | flops 671088640 | bytes 15892480 | tf_op jit(solution)/shard_map/ipcnk,dspn->ipcdsk/dot_general | solution.py:64
  212.8 1.7 fusion.43
  214.5 4.6 %fusion.35 = f32[2,2,32,16,256]{4,2,0,1,3:T(8,128)S(1)} fusion(bf16[16,5,2,256,128]{4,3,2,1,0:T(8,128)(2,1)S(1)} %bitcast.152, f32[16,5,1,32,128]{4,3,1,0,2:T(8,128)} %get-tuple-element.13, f32[16,5,1,32,128]{4,3,1,0,2:T(8,128)S(1)} %get-tuple-element.12, f32[16,5,128]{2,1,0:T(8,128)S(1)} %fusion.74), kind=kOutput, calls=%fused_computation.30 | convolution fusion | flops 673054720 | bytes 15245312 | tf_op jit(solution)/shard_map/ipcnk,ipdsk->cdsin/dot_general | solution.py:75
  221.6 34.7 %reduce-scatter.5.cloned.1.call-done = f32[2,32,512]{2,1,0:T(8,128)} async-done(((f32[2,32,4096]{2,1,0:T(8,128)}), f32[2,32,512]{2,1,0:T(8,128)}) %reduce-scatter.5.cloned.1.call-update) | async-done | bytes 131088 | tf_op jit(solution)/shard_map/reduce_scatter | solution.py:84
  256.2 1.1 multiply_reduce_fusion.2
  257.3 11.7 %psum.78 = f32[32]{0:T(128)S(1)} all-reduce(f32[32]{0:T(128)S(1)} %multiply_reduce_fusion.2), channel_id=1, replica_groups=mesh['col'=8,'row'=4] {'row'}, use_global_device_ids=true, to_apply=%region_16.0 | all-reduce | flops 32 | bytes 256 | tf_op jit(solution)/shard_map/psum | solution.py:11
  269.0 11.8 %psum.79 = f32[32]{0:T(128)S(1)} all-reduce(f32[32]{0:T(128)S(1)} %psum.78), channel_id=1, replica_groups=mesh['col'=8,'row'=4] {'col'}, use_global_device_ids=true, to_apply=%region_17.0 | all-reduce | flops 32 | bytes 256 | tf_op jit(solution)/shard_map/psum | solution.py:11
  281.7 10.1 %all_gather.14 = f32[2,8,10240]{2,1,0:T(8,128)S(1)} all-gather(f32[2,8,1280]{2,1,0:T(8,128)S(1)} %fusion.73), channel_id=1, replica_groups=mesh['col'=8,'row'=4] {'col'}, dimensions={2}, use_global_device_ids=true | all-gather | bytes 737280 | tf_op jit(solution)/shard_map/all_gather | solution.py:105
  292.4 14.8 %all_gather.15 = f32[2,32,1280]{2,1,0:T(8,128)S(1)} all-gather(f32[2,8,1280]{2,1,0:T(8,128)S(1)} %broadcast_select_fusion), channel_id=1, replica_groups=mesh['col'=8,'row'=4] {'row'}, dimensions={1}, use_global_device_ids=true | all-gather | bytes 409600 | tf_op jit(solution)/shard_map/all_gather | solution.py:108
  (94 shorter events, 13.7 us)
Async XLA Ops:
  7.2 63.5 %all-reduce.3.cloned.1.call-start = ((), (), s32[]{:S(2)}) async-start(), calls=%async_computation.2 | async-start | bytes 655360 | tf_op jit(solution)/shard_map/psum | solution.py:45
  26.0 0.7 copy-start.1
  32.7 1.3 copy-start
  33.9 99.8 %reduce-scatter.3.cloned.1.call-start = ((), (), s32[]{:S(2)}) async-start(), calls=%async_computation.3 | async-start | bytes 1179648 | tf_op jit(solution)/shard_map/reduce_scatter | solution.py:84
  83.7 8.4 %slice-start = ((s8[10485760]{0:T(1024)(128)(4,1)}), s8[2097152]{0:T(1024)(128)(4,1)S(1)}, s32[]{:S(2)}) async-start(s8[10485760]{0:T(1024)(128)(4,1)} %bitcast.149), calls=%async_computation.6 | async-start | bytes 4194304
  85.2 6.9 %slice-start.1 = ((s8[10485760]{0:T(1024)(128)(4,1)}), s8[4194304]{0:T(1024)(128)(4,1)S(1)}, s32[]{:S(2)}) async-start(s8[10485760]{0:T(1024)(128)(4,1)} %bitcast.149), calls=%async_computation.7 | async-start | bytes 8388608
  85.2 6.9 %slice-start.2 = ((s8[10485760]{0:T(1024)(128)(4,1)}), s8[4194304]{0:T(1024)(128)(4,1)S(1)}, s32[]{:S(2)}) async-start(s8[10485760]{0:T(1024)(128)(4,1)} %bitcast.149), calls=%async_computation.8 | async-start | bytes 8388608
  98.8 94.3 %all-reduce.5.cloned.1.call-start = ((), (), s32[]{:S(2)}) async-start(), calls=%async_computation.4 | async-start | bytes 655360 | tf_op jit(solution)/shard_map/psum | solution.py:45
  144.9 6.0 %slice-start.6 = ((s8[10485760]{0:T(1024)(128)(4,1)}), s8[4194304]{0:T(1024)(128)(4,1)S(1)}, s32[]{:S(2)}) async-start(s8[10485760]{0:T(1024)(128)(4,1)} %bitcast.153), calls=%async_computation.12 | async-start | bytes 8388608
  145.1 6.4 %slice-start.7 = ((s8[10485760]{0:T(1024)(128)(4,1)}), s8[4194304]{0:T(1024)(128)(4,1)S(1)}, s32[]{:S(2)}) async-start(s8[10485760]{0:T(1024)(128)(4,1)} %bitcast.153), calls=%async_computation.13 | async-start | bytes 8388608
  145.1 7.0 %slice-start.8 = ((s8[10485760]{0:T(1024)(128)(4,1)}), s8[2097152]{0:T(1024)(128)(4,1)S(1)}, s32[]{:S(2)}) async-start(s8[10485760]{0:T(1024)(128)(4,1)} %bitcast.153), calls=%async_computation.14 | async-start | bytes 4194304
  156.5 99.7 %reduce-scatter.5.cloned.1.call-start = ((), (), s32[]{:S(2)}) async-start(), calls=%async_computation.5 | async-start | bytes 1179648 | tf_op jit(solution)/shard_map/reduce_scatter | solution.py:84
  193.1 21.4 %slice-start.3 = ((s8[10485760]{0:T(1024)(128)(4,1)}), s8[2097152]{0:T(1024)(128)(4,1)S(1)}, s32[]{:S(2)}) async-start(s8[10485760]{0:T(1024)(128)(4,1)} %bitcast.151), calls=%async_computation.9 | async-start | bytes 4194304
  207.6 6.9 %slice-start.4 = ((s8[10485760]{0:T(1024)(128)(4,1)}), s8[4194304]{0:T(1024)(128)(4,1)S(1)}, s32[]{:S(2)}) async-start(s8[10485760]{0:T(1024)(128)(4,1)} %bitcast.151), calls=%async_computation.10 | async-start | bytes 8388608
  207.6 6.9 %slice-start.5 = ((s8[10485760]{0:T(1024)(128)(4,1)}), s8[4194304]{0:T(1024)(128)(4,1)S(1)}, s32[]{:S(2)}) async-start(s8[10485760]{0:T(1024)(128)(4,1)} %bitcast.151), calls=%async_computation.11 | async-start | bytes 8388608
  219.7 1.5 copy-start.2
Sparse Core Ops, SparseCore 0:
  34.0 36.5 all-reduce.2
  98.9 34.8 reduce-scatter.2
  156.6 36.4 all-reduce.4
  221.4 34.8 reduce-scatter.4
